TPU v7x, 512 devices: a whole 4x4x16 slice. The times are simulated.
512 devices in a mesh: dom: 128 (over z, x, core), tile: 4 (over y).
Axes of the slice: x: 4, y: 4, z: 16, core: 2. Of those that a mesh axis runs over, the one named last changes fastest.
Arguments:
- krylov_block: float32 [1536, 32, 128], P('dom'), may hold values from -6 to 6
- diag_block: float32 [1536, 128, 128], P(('dom', 'tile')), may hold values from -0.031819805 to 4.03182
- inverse_prev: float32 [1536, 128, 128], P(('dom', 'tile')), may hold values from -0.01767767 to 0.951011
- coupling_tiles: float32 [1536, 8, 128, 128], P('dom', 'tile'), may hold values from -0.14142136 to 0.14142136
- slot_kind: int32 [1536, 8], P('dom', 'tile'), may hold values from 0 to 2, as said below
- slot_link: int32 [1536, 8], P('dom', 'tile'), may hold values from 0 to 31, as said below
- send_slots: int32 [128, 4, 4, 4], P('dom', 'tile'), may hold values from 0 to 23, as said below
Outputs:
- inverse_new: float32 [1536, 128, 128], P(('dom', 'tile'))
- applied: float32 [1536, 32, 128], P('dom')
Inputs may be any that keep to these rules, and one draw needn't show every extreme that they name: `slot_kind`: every live slot has exactly one partner as stated, in the same tile group and in a partition at most two away; partners never lie outside the partitions 0 .. 127. `slot_link`: links of empty slots are 0. `send_slots`: entry [p, g, l, j] is a slot position of partition p in group g. Lists 0 and 1 name upper slots whose partners lie in partition p + 1 and p + 2, lists 2 and 3 lower slots whose partners lie in p - 1 and p - 2; the four lists and the partition's own pairs use distinct positions. Some list reaches 4 live entries in every draw.
All inputs are finite; a program needn't handle non-finite values.
Results may differ from a plain program's by a relative error of at most 0.0003.
Values sent between devices are 32-bit elements; how exact they have to be, the bound alone decides.
A program may use at most 64 MiB of HBM per device.

v0:
```python
import jax
import jax.numpy as jnp
from jax import lax
from jax.sharding import PartitionSpec as P

FSWEEPS = 2
LSWEEPS = 3
USWEEPS = 3


precise = lax.Precision.HIGHEST


def passed_along(block, axis, distance):
    devices = range(lax.axis_size(axis))
    route = [(i - distance, i) for i in devices if i - distance in devices]
    return lax.ppermute(block, axis, route)


def laid_out(blocks, dim):
    blocks = jnp.moveaxis(blocks, 0, dim)
    shape = blocks.shape
    return blocks.reshape(*shape[:dim], shape[dim] * shape[dim + 1], *shape[dim + 2 :])


def sent_to_all(value, axis):
    copies = jnp.broadcast_to(value, (lax.axis_size(axis), *value.shape))
    return lax.all_to_all(copies, axis, split_axis=0, concat_axis=0, tiled=True)


def collect(value, axis, dim):
    return laid_out(sent_to_all(value, axis), dim)


def in_blocks(value, dim, devices):
    shape = value.shape
    blocks = value.reshape(*shape[:dim], devices, shape[dim] // devices, *shape[dim + 1 :])
    return jnp.moveaxis(blocks, dim, 0)


def sum_at_owner(value, axis, dim):
    devices = lax.axis_size(axis)
    blocks = lax.all_to_all(in_blocks(value, dim, devices), axis, 0, 0, tiled=True)
    return jnp.sum(blocks, axis=0)


def over_copies(value, axis):
    everything = sent_to_all(value, axis)
    return jnp.sum(everything, axis=0)


def newton_step(inverse, pivot):
    product = jnp.matmul(inverse, pivot, precision=precise)
    return 2.0 * inverse - jnp.matmul(product, inverse, precision=precise)


def apply_inverse(inverse, vectors):
    return jnp.einsum("rvj,rij->rvi", vectors, inverse, precision=precise)


def local(krylov_block, diag_block, inverse_prev, coupling_tiles, slot_kind, slot_link, send_slots):
    row_count = coupling_tiles.shape[0]
    slot_width = coupling_tiles.shape[1]
    block_size = coupling_tiles.shape[2]
    slot_total = row_count * slot_width
    capacity = send_slots.shape[3]
    partner = slot_link.reshape(slot_total)
    send_table = send_slots.reshape(4, capacity)
    send_rows = send_table // slot_width
    row_source = jnp.where(
        partner < slot_total, partner // slot_width, partner - slot_total + row_count
    )
    tiles_lower = coupling_tiles * (slot_kind == 1).astype(jnp.float32)[:, :, None, None]
    tiles_upper = coupling_tiles * (slot_kind == 2).astype(jnp.float32)[:, :, None, None]

    def spread(inverse_mine):
        return collect(inverse_mine, "tile", 0)

    inverse_mine = inverse_prev
    inverse_all = spread(inverse_mine)
    for sweep_no in range(FSWEEPS):
        upper_products = jnp.einsum("rij,rwjk->rwik", inverse_all, tiles_upper, precision=precise)
        upper_products = upper_products.reshape(slot_total, block_size, block_size)
        near_out = upper_products[send_table[0]]
        far_out = upper_products[send_table[1]]
        pivot_near_in = passed_along(near_out, "dom", 1)
        pivot_far_in = passed_along(far_out, "dom", 2)
        pivot_lookup = jnp.concatenate([upper_products, pivot_near_in, pivot_far_in], 0)
        pivot_gathered = pivot_lookup[partner].reshape(
            row_count, slot_width, block_size, block_size
        )
        shares = sum_at_owner(
            jnp.einsum("rwij,rwjk->rik", tiles_lower, pivot_gathered, precision=precise), "tile", 0
        )
        inverse_mine = newton_step(inverse_mine, diag_block - shares)
        inverse_all = spread(inverse_mine)
    slot_shape = (row_count, slot_width) + krylov_block.shape[1:]
    lower_y = krylov_block
    for sweep_no in range(LSWEEPS):
        scaled = apply_inverse(inverse_all, lower_y)
        near_in = passed_along(scaled[send_rows[0]], "dom", 1)
        far_in = passed_along(scaled[send_rows[1]], "dom", 2)
        lookup = jnp.concatenate([scaled, near_in, far_in], 0)
        gathered = lookup[row_source].reshape(slot_shape)
        partial_value = jnp.einsum("rwvj,rwij->rvi", gathered, tiles_lower, precision=precise)
        lower_y = krylov_block - over_copies(partial_value, "tile")
    solved = apply_inverse(inverse_all, lower_y)
    for sweep_no in range(USWEEPS):
        near_in = passed_along(solved[send_rows[2]], "dom", -1)
        far_in = passed_along(solved[send_rows[3]], "dom", -2)
        lookup = jnp.concatenate([solved, near_in, far_in], 0)
        gathered = lookup[row_source].reshape(slot_shape)
        partial_value = jnp.einsum("rwvj,rwij->rvi", gathered, tiles_upper, precision=precise)
        solved = apply_inverse(inverse_all, lower_y - over_copies(partial_value, "tile"))
    return (inverse_mine, solved)


def solution(mesh):
    placed = (
        P("dom", None, None),
        P(("dom", "tile"), None, None),
        P(("dom", "tile"), None, None),
        P("dom", "tile", None, None),
        P("dom", "tile"),
        P("dom", "tile"),
        P("dom", "tile", None, None),
    )
    return jax.shard_map(
        local,
        mesh=mesh,
        in_specs=placed,
        out_specs=(P(("dom", "tile"), None, None), P("dom", None, None)),
        check_vma=False,
    )
```

profile of v0, /device:TPU:230, one launch (start us, length us, event | category | flops | bytes accessed | tf_op | source)
XLA Modules:
  0.0 329.5 jit_solution(5710893002090708309)
XLA Ops:
  0.7 2.0 broadcast_in_dim.18
  2.7 4.5 %all-to-all-start = ((f32[4,3,128,128]{3,2,1,0:T(8,128)}), f32[4,3,128,128]{3,2,1,0:T(8,128)}, u32[]{:S(2)}, u32[]{:S(2)}) async-start(f32[4,3,128,128]{3,2,1,0:T(8,128)} %broadcast_in_dim.18), calls=%async_computation | async-start | bytes 1572864 | tf_op jit(solution)/shard_map/all_to_all | solution.py:28
  7.6 11.9 %all-to-all-done = f32[4,3,128,128]{3,2,1,0:T(8,128)} async-done(((f32[4,3,128,128]{3,2,1,0:T(8,128)}), f32[4,3,128,128]{3,2,1,0:T(8,128)}, u32[]{:S(2)}, u32[]{:S(2)}) %all-to-all-start) | async-done | bytes 786464 | tf_op jit(solution)/shard_map/all_to_all | solution.py:28
  19.6 4.0 %fusion.8 = f32[12,2,128,128]{3,2,1,0:T(8,128)S(1)} fusion(f32[12,128,128,1]{2,1,3,0:T(8,128)} %bitcast.2, f32[12,2,128,128]{3,2,1,0:T(8,128)S(1)} %copy-done, f32[12,2]{1,0:T(8,128)S(1)} %copy.24), kind=kOutput, calls=%fused_computation.34 | convolution fusion | flops 604372992 | bytes 3932256 | tf_op jit(solution)/shard_map/rij,rwjk->rwik/dot_general | solution.py:82
  23.6 1.3 gather_fusion
  24.9 1.9 collective-permute-start
  26.8 1.3 gather_fusion.1
  28.1 4.9 %collective-permute-start.1 = (f32[4,128,128]{1,2,0:T(8,128)}, f32[4,128,128]{1,2,0:T(8,128)S(1)}, u32[]{:S(2)}, u32[]{:S(2)}) collective-permute-start(f32[4,128,128]{1,2,0:T(8,128)} %gather_fusion.1), channel_id=1, source_target_pairs={{0,8},{4,12},{8,16},{12,20},{16,24},{20,28},{24,32},{28,36},{32,40... | collective-permute-start | bytes 786440 | tf_op jit(solution)/shard_map/ppermute | solution.py:17
  33.6 5.8 %collective-permute-done.1 = f32[4,128,128]{1,2,0:T(8,128)S(1)} collective-permute-done((f32[4,128,128]{1,2,0:T(8,128)}, f32[4,128,128]{1,2,0:T(8,128)S(1)}, u32[]{:S(2)}, u32[]{:S(2)}) %collective-permute-start.1) | collective-permute-done | bytes 262176 | tf_op jit(solution)/shard_map/ppermute | solution.py:17
  39.4 1.5 pad_maximum_fusion
  40.9 2.2 gather_fusion.2
  43.1 1.7 fusion.18
  44.8 16.0 %all_to_all.55 = f32[4,3,128,128]{3,2,1,0:T(8,128)S(1)} all-to-all(f32[4,3,128,128]{3,2,1,0:T(8,128)S(1)} %bitcast.139), channel_id=1, replica_groups=mesh['dom'=128,'tile'=4] {'tile'}, dimensions={0} | all-to-all | bytes 1572864 | tf_op jit(solution)/shard_map/all_to_all | solution.py:43
  61.7 15.0 %all_to_all.56 = f32[4,3,128,128]{3,2,1,0:T(8,128)S(1)} all-to-all(f32[4,3,128,128]{3,2,1,0:T(8,128)S(1)} %broadcast_in_dim.19), channel_id=1, replica_groups=mesh['dom'=128,'tile'=4] {'tile'}, dimensions={0} | all-to-all | bytes 1572864 | tf_op jit(solution)/shard_map/all_to_all | solution.py:28
  76.7 2.9 fusion.6
  79.6 1.4 gather_fusion.3
  81.0 1.4 gather_fusion.4
  82.4 1.9 collective-permute-start.2
  84.3 6.7 %collective-permute-start.3 = (f32[4,128,128]{1,2,0:T(8,128)}, f32[4,128,128]{1,2,0:T(8,128)S(1)}, u32[]{:S(2)}, u32[]{:S(2)}) collective-permute-start(f32[4,128,128]{1,2,0:T(8,128)} %gather_fusion.4), channel_id=1, source_target_pairs={{0,8},{4,12},{8,16},{12,20},{16,24},{20,28},{24,32},{28,36},{32,40... | collective-permute-start | bytes 786440 | tf_op jit(solution)/shard_map/ppermute | solution.py:17
  91.0 7.0 %collective-permute-done.3 = f32[4,128,128]{1,2,0:T(8,128)S(1)} collective-permute-done((f32[4,128,128]{1,2,0:T(8,128)}, f32[4,128,128]{1,2,0:T(8,128)S(1)}, u32[]{:S(2)}, u32[]{:S(2)}) %collective-permute-start.3) | collective-permute-done | bytes 262176 | tf_op jit(solution)/shard_map/ppermute | solution.py:17
  98.0 1.5 pad_maximum_fusion.1
  99.5 2.4 gather_fusion.5
  101.9 1.7 fusion.16
  103.6 15.6 %all_to_all.57 = f32[4,3,128,128]{3,2,1,0:T(8,128)S(1)} all-to-all(f32[4,3,128,128]{3,2,1,0:T(8,128)S(1)} %bitcast.141), channel_id=1, replica_groups=mesh['dom'=128,'tile'=4] {'tile'}, dimensions={0} | all-to-all | bytes 1572864 | tf_op jit(solution)/shard_map/all_to_all | solution.py:43
  120.9 3.6 %all-to-all-start.4 = ((f32[4,3,128,128]{3,2,1,0:T(8,128)}), f32[4,3,128,128]{3,2,1,0:T(8,128)S(1)}, u32[]{:S(2)}, u32[]{:S(2)}) async-start(f32[4,3,128,128]{3,2,1,0:T(8,128)} %broadcast_in_dim.20), calls=%async_computation.4 | async-start | bytes 1572864 | tf_op jit(solution)/shard_map/all_to_all | solution.py:28
  125.1 11.3 %all-to-all-done.4 = f32[4,3,128,128]{3,2,1,0:T(8,128)S(1)} async-done(((f32[4,3,128,128]{3,2,1,0:T(8,128)}), f32[4,3,128,128]{3,2,1,0:T(8,128)S(1)}, u32[]{:S(2)}, u32[]{:S(2)}) %all-to-all-start.4) | async-done | bytes 786464 | tf_op jit(solution)/shard_map/all_to_all | solution.py:28
  136.5 1.3 convolution_bitcast_fusion
  138.4 1.9 collective-permute-start.4
  140.9 7.3 %collective-permute-start.5 = (f32[4,32,128]{2,1,0:T(8,128)S(1)}, f32[4,32,128]{2,1,0:T(8,128)S(1)}, u32[]{:S(2)}, u32[]{:S(2)}) collective-permute-start(f32[4,32,128]{2,1,0:T(8,128)S(1)} %gather_fusion.7), channel_id=1, source_target_pairs={{0,8},{4,12},{8,16},{12,20},{16,24},{20,28},{24,32},{28,36},{32,40... | collective-permute-start | bytes 196616 | tf_op jit(solution)/shard_map/ppermute | solution.py:17
  148.2 1.8 collective-permute-done.5
  150.7 1.7 fusion.20
  152.4 15.8 %all_to_all.58 = f32[4,12,32,128]{3,2,1,0:T(8,128)S(1)} all-to-all(f32[4,12,32,128]{3,2,1,0:T(8,128)S(1)} %broadcast_in_dim.21), channel_id=1, replica_groups=mesh['dom'=128,'tile'=4] {'tile'}, dimensions={0} | all-to-all | bytes 1572864 | tf_op jit(solution)/shard_map/all_to_all | solution.py:28
  168.3 1.3 fusion.56
  171.0 2.1 collective-permute-start.6
  173.1 6.5 %collective-permute-start.7 = (f32[4,32,128]{2,1,0:T(8,128)S(1)}, f32[4,32,128]{2,1,0:T(8,128)S(1)}, u32[]{:S(2)}, u32[]{:S(2)}) collective-permute-start(f32[4,32,128]{2,1,0:T(8,128)S(1)} %gather_fusion.10), channel_id=1, source_target_pairs={{0,8},{4,12},{8,16},{12,20},{16,24},{20,28},{24,32},{28,36},{32,40... | collective-permute-start | bytes 196616 | tf_op jit(solution)/shard_map/ppermute | solution.py:17
  179.6 1.9 collective-permute-done.7
  182.2 1.7 fusion.23
  183.9 15.8 %all_to_all.59 = f32[4,12,32,128]{3,2,1,0:T(8,128)S(1)} all-to-all(f32[4,12,32,128]{3,2,1,0:T(8,128)S(1)} %broadcast_in_dim.22), channel_id=1, replica_groups=mesh['dom'=128,'tile'=4] {'tile'}, dimensions={0} | all-to-all | bytes 1572864 | tf_op jit(solution)/shard_map/all_to_all | solution.py:28
  199.7 1.3 fusion.54
  202.4 2.1 collective-permute-start.8
  204.5 6.5 %collective-permute-start.9 = (f32[4,32,128]{2,1,0:T(8,128)S(1)}, f32[4,32,128]{2,1,0:T(8,128)S(1)}, u32[]{:S(2)}, u32[]{:S(2)}) collective-permute-start(f32[4,32,128]{2,1,0:T(8,128)S(1)} %gather_fusion.13), channel_id=1, source_target_pairs={{0,8},{4,12},{8,16},{12,20},{16,24},{20,28},{24,32},{28,36},{32,40... | collective-permute-start | bytes 196616 | tf_op jit(solution)/shard_map/ppermute | solution.py:17
  211.0 1.9 collective-permute-done.9
  213.6 1.7 fusion.26
  216.3 3.5 %all-to-all-start.7 = ((f32[4,12,32,128]{3,2,1,0:T(8,128)}), f32[4,12,32,128]{3,2,1,0:T(8,128)S(1)}, u32[]{:S(2)}, u32[]{:S(2)}) async-start(f32[4,12,32,128]{3,2,1,0:T(8,128)} %broadcast_in_dim.23), calls=%async_computation.7 | async-start | bytes 1572864 | tf_op jit(solution)/shard_map/all_to_all | solution.py:28
  219.8 13.3 %all-to-all-done.7 = f32[4,12,32,128]{3,2,1,0:T(8,128)S(1)} async-done(((f32[4,12,32,128]{3,2,1,0:T(8,128)}), f32[4,12,32,128]{3,2,1,0:T(8,128)S(1)}, u32[]{:S(2)}, u32[]{:S(2)}) %all-to-all-start.7) | async-done | bytes 786464 | tf_op jit(solution)/shard_map/all_to_all | solution.py:28
  233.2 1.3 fusion.73
  235.1 1.9 collective-permute-start.10
  237.6 1.9 collective-permute-start.11
  239.5 7.8 %collective-permute-done.11 = f32[4,32,128]{2,1,0:T(8,128)S(1)} collective-permute-done((f32[4,32,128]{2,1,0:T(8,128)S(1)}, f32[4,32,128]{2,1,0:T(8,128)S(1)}, u32[]{:S(2)}, u32[]{:S(2)}) %collective-permute-start.11) | collective-permute-done | bytes 65568 | tf_op jit(solution)/shard_map/ppermute | solution.py:17
  248.0 1.7 fusion.29
  249.8 14.8 %all_to_all.60 = f32[4,12,32,128]{3,2,1,0:T(8,128)S(1)} all-to-all(f32[4,12,32,128]{3,2,1,0:T(8,128)S(1)} %broadcast_in_dim.24), channel_id=1, replica_groups=mesh['dom'=128,'tile'=4] {'tile'}, dimensions={0} | all-to-all | bytes 1572864 | tf_op jit(solution)/shard_map/all_to_all | solution.py:28
  264.6 1.3 fusion.52
  267.1 1.9 collective-permute-start.12
  269.0 2.1 collective-permute-start.13
  271.2 7.5 %collective-permute-done.13 = f32[4,32,128]{2,1,0:T(8,128)S(1)} collective-permute-done((f32[4,32,128]{2,1,0:T(8,128)S(1)}, f32[4,32,128]{2,1,0:T(8,128)S(1)}, u32[]{:S(2)}, u32[]{:S(2)}) %collective-permute-start.13) | collective-permute-done | bytes 65568 | tf_op jit(solution)/shard_map/ppermute | solution.py:17
  279.5 1.7 fusion.32
  281.2 14.8 %all_to_all.61 = f32[4,12,32,128]{3,2,1,0:T(8,128)S(1)} all-to-all(f32[4,12,32,128]{3,2,1,0:T(8,128)S(1)} %broadcast_in_dim.25), channel_id=1, replica_groups=mesh['dom'=128,'tile'=4] {'tile'}, dimensions={0} | all-to-all | bytes 1572864 | tf_op jit(solution)/shard_map/all_to_all | solution.py:28
  296.1 1.3 fusion.50
  298.5 1.9 collective-permute-start.14
  300.4 1.9 collective-permute-start.15
  302.4 7.8 %collective-permute-done.15 = f32[4,32,128]{2,1,0:T(8,128)S(1)} collective-permute-done((f32[4,32,128]{2,1,0:T(8,128)S(1)}, f32[4,32,128]{2,1,0:T(8,128)S(1)}, u32[]{:S(2)}, u32[]{:S(2)}) %collective-permute-start.15) | collective-permute-done | bytes 65568 | tf_op jit(solution)/shard_map/ppermute | solution.py:17
  310.9 1.7 fusion.35
  312.6 14.8 %all_to_all.62 = f32[4,12,32,128]{3,2,1,0:T(8,128)S(1)} all-to-all(f32[4,12,32,128]{3,2,1,0:T(8,128)S(1)} %broadcast_in_dim.26), channel_id=1, replica_groups=mesh['dom'=128,'tile'=4] {'tile'}, dimensions={0} | all-to-all | bytes 1572864 | tf_op jit(solution)/shard_map/all_to_all | solution.py:28
  327.5 2.0 fusion.48
  (106 shorter events, 17.4 us)
Async XLA Ops:
  0.6 6.5 %copy-start.15 = (s32[12,2]{0,1:T(2,128)S(1)}, s32[12,2]{0,1:T(2,128)}, u32[]{:S(2)}) copy-start(s32[12,2]{0,1:T(2,128)} %param.11) | copy-start | bytes 292
  0.6 6.6 %copy-start.16 = (s32[12,2]{0,1:T(2,128)S(1)}, s32[12,2]{0,1:T(2,128)}, u32[]{:S(2)}) copy-start(s32[12,2]{0,1:T(2,128)} %param.12) | copy-start | bytes 292
  0.7 6.9 %copy-start.11 = (s32[1,1,4,4]{3,2,1,0:T(4,128)S(1)}, s32[1,1,4,4]{3,2,1,0:T(4,128)}, u32[]{:S(2)}) copy-start(s32[1,1,4,4]{3,2,1,0:T(4,128)} %param.13) | copy-start | bytes 196
  0.7 18.9 %copy-start = (f32[12,2,128,128]{3,2,1,0:T(8,128)S(1)}, f32[12,2,128,128]{3,2,1,0:T(8,128)}, u32[]{:S(2)}) copy-start(f32[12,2,128,128]{3,2,1,0:T(8,128)} %param.10) | copy-start | bytes 4718596
  2.7 16.9 %all-to-all-start = ((f32[4,3,128,128]{3,2,1,0:T(8,128)}), f32[4,3,128,128]{3,2,1,0:T(8,128)}, u32[]{:S(2)}, u32[]{:S(2)}) async-start(f32[4,3,128,128]{3,2,1,0:T(8,128)} %broadcast_in_dim.18), calls=%async_computation | async-start | bytes 1572864 | tf_op jit(solution)/shard_map/all_to_all | solution.py:28
  7.6 16.0 %copy-start.8 = (s32[1024]{0:T(1024)}, s32[1024]{0:T(1024)S(1)}, u32[]{:S(2)}) copy-start(s32[1024]{0:T(1024)S(1)} %pad_clamp_fusion.7) | copy-start | bytes 12292
  7.6 19.2 %copy-start.9 = (s32[1024]{0:T(1024)}, s32[1024]{0:T(1024)S(1)}, u32[]{:S(2)}) copy-start(s32[1024]{0:T(1024)S(1)} %pad_clamp_fusion.6) | copy-start | bytes 12292
  24.9 8.7 %collective-permute-start = (f32[4,128,128]{1,2,0:T(8,128)}, f32[4,128,128]{1,2,0:T(8,128)S(1)}, u32[]{:S(2)}, u32[]{:S(2)}) collective-permute-start(f32[4,128,128]{1,2,0:T(8,128)} %gather_fusion), channel_id=1, source_target_pairs={{0,4},{4,8},{8,12},{12,16},{16,20},{20,24},{24,28},{28,32},{32,36}... | collective-permute-start | bytes 786440 | tf_op jit(solution)/shard_map/ppermute | solution.py:17
  28.1 11.3 %collective-permute-start.1 = (f32[4,128,128]{1,2,0:T(8,128)}, f32[4,128,128]{1,2,0:T(8,128)S(1)}, u32[]{:S(2)}, u32[]{:S(2)}) collective-permute-start(f32[4,128,128]{1,2,0:T(8,128)} %gather_fusion.1), channel_id=1, source_target_pairs={{0,8},{4,12},{8,16},{12,20},{16,24},{20,28},{24,32},{28,36},{32,40... | collective-permute-start | bytes 786440 | tf_op jit(solution)/shard_map/ppermute | solution.py:17
  33.6 7.3 %copy-start.10 = (s32[1024]{0:T(1024)}, s32[1024]{0:T(1024)S(1)}, u32[]{:S(2)}) copy-start(s32[1024]{0:T(1024)S(1)} %pad_clamp_fusion.5) | copy-start | bytes 12292
  44.8 16.1 %copy-start.2 = (f32[3,128,128]{2,1,0:T(8,128)S(1)}, f32[3,128,128]{2,1,0:T(8,128)}, u32[]{:S(2)}) copy-start(f32[3,128,128]{2,1,0:T(8,128)} %param.9) | copy-start | bytes 589828
  44.8 16.1 %copy-start.3 = (f32[3,128,128]{2,1,0:T(8,128)S(1)}, f32[3,128,128]{2,1,0:T(8,128)}, u32[]{:S(2)}) copy-start(f32[3,128,128]{2,1,0:T(8,128)} %param.8) | copy-start | bytes 589828
  82.4 8.6 %collective-permute-start.2 = (f32[4,128,128]{1,2,0:T(8,128)}, f32[4,128,128]{1,2,0:T(8,128)S(1)}, u32[]{:S(2)}, u32[]{:S(2)}) collective-permute-start(f32[4,128,128]{1,2,0:T(8,128)} %gather_fusion.3), channel_id=1, source_target_pairs={{0,4},{4,8},{8,12},{12,16},{16,20},{20,24},{24,28},{28,32},{32,36}... | collective-permute-start | bytes 786440 | tf_op jit(solution)/shard_map/ppermute | solution.py:17
  84.3 13.7 %collective-permute-start.3 = (f32[4,128,128]{1,2,0:T(8,128)}, f32[4,128,128]{1,2,0:T(8,128)S(1)}, u32[]{:S(2)}, u32[]{:S(2)}) collective-permute-start(f32[4,128,128]{1,2,0:T(8,128)} %gather_fusion.4), channel_id=1, source_target_pairs={{0,8},{4,12},{8,16},{12,20},{16,24},{20,28},{24,32},{28,36},{32,40... | collective-permute-start | bytes 786440 | tf_op jit(solution)/shard_map/ppermute | solution.py:17
  119.5 5.0 %copy-start.12 = (s32[1,1,4,4]{3,2,1,0:T(4,128)S(1)}, s32[1,1,4,4]{3,2,1,0:T(4,128)}, u32[]{:S(2)}) copy-start(s32[1,1,4,4]{3,2,1,0:T(4,128)} %param.13) | copy-start | bytes 196
  119.5 16.9 %copy-start.1 = (f32[12,32,128]{2,1,0:T(8,128)S(1)}, f32[12,32,128]{2,1,0:T(8,128)}, u32[]{:S(2)}) copy-start(f32[12,32,128]{2,1,0:T(8,128)} %param.7) | copy-start | bytes 589828
  119.9 16.6 %copy-start.4 = (f32[3,128,128]{2,1,0:T(8,128)}, f32[3,128,128]{2,1,0:T(8,128)S(1)}, u32[]{:S(2)}) copy-start(f32[3,128,128]{2,1,0:T(8,128)S(1)} %convolution_subtract_fusion) | copy-start | bytes 589828
  120.9 27.3 %copy-start.17 = (s32[24]{0:T(128)S(1)}, s32[24]{0:T(128)}, u32[]{:S(2)}) copy-start(s32[24]{0:T(128)} %get-tuple-element.10) | copy-start | bytes 292
  120.9 15.6 %all-to-all-start.4 = ((f32[4,3,128,128]{3,2,1,0:T(8,128)}), f32[4,3,128,128]{3,2,1,0:T(8,128)S(1)}, u32[]{:S(2)}, u32[]{:S(2)}) async-start(f32[4,3,128,128]{3,2,1,0:T(8,128)} %broadcast_in_dim.20), calls=%async_computation.4 | async-start | bytes 1572864 | tf_op jit(solution)/shard_map/all_to_all | solution.py:28
  125.1 12.7 %copy-start.6 = (s32[1024]{0:T(1024)}, s32[1024]{0:T(1024)S(1)}, u32[]{:S(2)}) copy-start(s32[1024]{0:T(1024)S(1)} %pad_clamp_fusion.4) | copy-start | bytes 12292
  125.1 15.2 %copy-start.7 = (s32[1024]{0:T(1024)}, s32[1024]{0:T(1024)S(1)}, u32[]{:S(2)}) copy-start(s32[1024]{0:T(1024)S(1)} %pad_clamp_fusion.3) | copy-start | bytes 12292
  138.4 9.9 %collective-permute-start.4 = (f32[4,32,128]{2,1,0:T(8,128)S(1)}, f32[4,32,128]{2,1,0:T(8,128)S(1)}, u32[]{:S(2)}, u32[]{:S(2)}) collective-permute-start(f32[4,32,128]{2,1,0:T(8,128)S(1)} %gather_fusion.6), channel_id=1, source_target_pairs={{0,4},{4,8},{8,12},{12,16},{16,20},{20,24},{24,28},{28,32},{32,36}... | collective-permute-start | bytes 196616 | tf_op jit(solution)/shard_map/ppermute | solution.py:17
  140.9 9.2 %collective-permute-start.5 = (f32[4,32,128]{2,1,0:T(8,128)S(1)}, f32[4,32,128]{2,1,0:T(8,128)S(1)}, u32[]{:S(2)}, u32[]{:S(2)}) collective-permute-start(f32[4,32,128]{2,1,0:T(8,128)S(1)} %gather_fusion.7), channel_id=1, source_target_pairs={{0,8},{4,12},{8,16},{12,20},{16,24},{20,28},{24,32},{28,36},{32,40... | collective-permute-start | bytes 196616 | tf_op jit(solution)/shard_map/ppermute | solution.py:17
  148.2 4.1 %copy-start.5 = (s32[1024]{0:T(1024)}, s32[1024]{0:T(1024)S(1)}, u32[]{:S(2)}) copy-start(s32[1024]{0:T(1024)S(1)} %pad_clamp_fusion.2) | copy-start | bytes 12292
  171.0 8.6 %collective-permute-start.6 = (f32[4,32,128]{2,1,0:T(8,128)S(1)}, f32[4,32,128]{2,1,0:T(8,128)S(1)}, u32[]{:S(2)}, u32[]{:S(2)}) collective-permute-start(f32[4,32,128]{2,1,0:T(8,128)S(1)} %gather_fusion.9), channel_id=1, source_target_pairs={{0,4},{4,8},{8,12},{12,16},{16,20},{20,24},{24,28},{28,32},{32,36}... | collective-permute-start | bytes 196616 | tf_op jit(solution)/shard_map/ppermute | solution.py:17
  173.1 8.4 %collective-permute-start.7 = (f32[4,32,128]{2,1,0:T(8,128)S(1)}, f32[4,32,128]{2,1,0:T(8,128)S(1)}, u32[]{:S(2)}, u32[]{:S(2)}) collective-permute-start(f32[4,32,128]{2,1,0:T(8,128)S(1)} %gather_fusion.10), channel_id=1, source_target_pairs={{0,8},{4,12},{8,16},{12,20},{16,24},{20,28},{24,32},{28,36},{32,40... | collective-permute-start | bytes 196616 | tf_op jit(solution)/shard_map/ppermute | solution.py:17
  202.4 8.6 %collective-permute-start.8 = (f32[4,32,128]{2,1,0:T(8,128)S(1)}, f32[4,32,128]{2,1,0:T(8,128)S(1)}, u32[]{:S(2)}, u32[]{:S(2)}) collective-permute-start(f32[4,32,128]{2,1,0:T(8,128)S(1)} %gather_fusion.12), channel_id=1, source_target_pairs={{0,4},{4,8},{8,12},{12,16},{16,20},{20,24},{24,28},{28,32},{32,36}... | collective-permute-start | bytes 196616 | tf_op jit(solution)/shard_map/ppermute | solution.py:17
  204.5 8.4 %collective-permute-start.9 = (f32[4,32,128]{2,1,0:T(8,128)S(1)}, f32[4,32,128]{2,1,0:T(8,128)S(1)}, u32[]{:S(2)}, u32[]{:S(2)}) collective-permute-start(f32[4,32,128]{2,1,0:T(8,128)S(1)} %gather_fusion.13), channel_id=1, source_target_pairs={{0,8},{4,12},{8,16},{12,20},{16,24},{20,28},{24,32},{28,36},{32,40... | collective-permute-start | bytes 196616 | tf_op jit(solution)/shard_map/ppermute | solution.py:17
  215.3 4.5 %copy-start.14 = (s32[4]{0:T(128)S(1)}, s32[4]{0:T(128)}, u32[]{:S(2)}) copy-start(s32[4]{0:T(128)} %get-tuple-element.2) | copy-start | bytes 52
  215.3 4.5 %copy-start.13 = (s32[4]{0:T(128)S(1)}, s32[4]{0:T(128)}, u32[]{:S(2)}) copy-start(s32[4]{0:T(128)} %get-tuple-element.3) | copy-start | bytes 52
  216.3 16.8 %all-to-all-start.7 = ((f32[4,12,32,128]{3,2,1,0:T(8,128)}), f32[4,12,32,128]{3,2,1,0:T(8,128)S(1)}, u32[]{:S(2)}, u32[]{:S(2)}) async-start(f32[4,12,32,128]{3,2,1,0:T(8,128)} %broadcast_in_dim.23), calls=%async_computation.7 | async-start | bytes 1572864 | tf_op jit(solution)/shard_map/all_to_all | solution.py:28
  235.1 4.4 %collective-permute-start.10 = (f32[4,32,128]{2,1,0:T(8,128)S(1)}, f32[4,32,128]{2,1,0:T(8,128)S(1)}, u32[]{:S(2)}, u32[]{:S(2)}) collective-permute-start(f32[4,32,128]{2,1,0:T(8,128)S(1)} %gather_fusion.15), channel_id=1, source_target_pairs={{4,0},{8,4},{12,8},{16,12},{20,16},{24,20},{28,24},{32,28},{36,32}... | collective-permute-start | bytes 196616 | tf_op jit(solution)/shard_map/ppermute | solution.py:17
  237.6 9.7 %collective-permute-start.11 = (f32[4,32,128]{2,1,0:T(8,128)S(1)}, f32[4,32,128]{2,1,0:T(8,128)S(1)}, u32[]{:S(2)}, u32[]{:S(2)}) collective-permute-start(f32[4,32,128]{2,1,0:T(8,128)S(1)} %gather_fusion.16), channel_id=1, source_target_pairs={{8,0},{12,4},{16,8},{20,12},{24,16},{28,20},{32,24},{36,28},{40,32... | collective-permute-start | bytes 196616 | tf_op jit(solution)/shard_map/ppermute | solution.py:17
  267.1 4.1 %collective-permute-start.12 = (f32[4,32,128]{2,1,0:T(8,128)S(1)}, f32[4,32,128]{2,1,0:T(8,128)S(1)}, u32[]{:S(2)}, u32[]{:S(2)}) collective-permute-start(f32[4,32,128]{2,1,0:T(8,128)S(1)} %gather_fusion.18), channel_id=1, source_target_pairs={{4,0},{8,4},{12,8},{16,12},{20,16},{24,20},{28,24},{32,28},{36,32}... | collective-permute-start | bytes 196616 | tf_op jit(solution)/shard_map/ppermute | solution.py:17
  269.0 9.7 %collective-permute-start.13 = (f32[4,32,128]{2,1,0:T(8,128)S(1)}, f32[4,32,128]{2,1,0:T(8,128)S(1)}, u32[]{:S(2)}, u32[]{:S(2)}) collective-permute-start(f32[4,32,128]{2,1,0:T(8,128)S(1)} %gather_fusion.19), channel_id=1, source_target_pairs={{8,0},{12,4},{16,8},{20,12},{24,16},{28,20},{32,24},{36,28},{40,32... | collective-permute-start | bytes 196616 | tf_op jit(solution)/shard_map/ppermute | solution.py:17
  298.5 3.9 %collective-permute-start.14 = (f32[4,32,128]{2,1,0:T(8,128)S(1)}, f32[4,32,128]{2,1,0:T(8,128)S(1)}, u32[]{:S(2)}, u32[]{:S(2)}) collective-permute-start(f32[4,32,128]{2,1,0:T(8,128)S(1)} %gather_fusion.21), channel_id=1, source_target_pairs={{4,0},{8,4},{12,8},{16,12},{20,16},{24,20},{28,24},{32,28},{36,32}... | collective-permute-start | bytes 196616 | tf_op jit(solution)/shard_map/ppermute | solution.py:17
  300.4 9.7 %collective-permute-start.15 = (f32[4,32,128]{2,1,0:T(8,128)S(1)}, f32[4,32,128]{2,1,0:T(8,128)S(1)}, u32[]{:S(2)}, u32[]{:S(2)}) collective-permute-start(f32[4,32,128]{2,1,0:T(8,128)S(1)} %gather_fusion.22), channel_id=1, source_target_pairs={{8,0},{12,4},{16,8},{20,12},{24,16},{28,20},{32,24},{36,28},{40,32... | collective-permute-start | bytes 196616 | tf_op jit(solution)/shard_map/ppermute | solution.py:17
where the time goes:
time: 331 us; the launch traced here: 329 us
  blocking collectives  122 us (37%)
  waiting for transfers between devices  78 us (24%)
  starting transfers between devices  65.1 us (20%)
  matrix products  31.5 us (10%)
  local copies, waits for them, and re-layouts  26.1 us (8%)
  other arithmetic  4.83 us (1%)
    all_to_all x6, blocking collectives, sent_to_all(): return lax.all_to_all(copies, axis, split_axis=0, concat_axis=0, tiled=True)  90.9 us
    ppermute x16, starting transfers between devices, passed_along(): return lax.ppermute(block, axis, route)  53.5 us
    ppermute x16, waiting for transfers between devices, passed_along(): return lax.ppermute(block, axis, route)  41.5 us
    all_to_all x3, waiting for transfers between devices, sent_to_all(): return lax.all_to_all(copies, axis, split_axis=0, concat_axis=0, tiled=True)  36.5 us
    all_to_all x2, blocking collectives, sum_at_owner(): lax.all_to_all(in_blocks(value, dim, devices), axis, 0, 0, tiled=True)  31.6 us
    all_to_all x3, starting transfers between devices, sent_to_all(): return lax.all_to_all(copies, axis, split_axis=0, concat_axis=0, tiled=True)  11.6 us
    dot_general x7, matrix products, apply_inverse(): return jnp.einsum('rvj,rij->rvi', vectors, inverse, precision=precise)  9.93 us
    dot_general x2, matrix products, local(): jnp.einsum('rij,rwjk->rwik', inverse_all, tiles_upper, precision=precise)  6.95 us
  transfers between devices with their start and end apart: 19, of which 11 were waited for; matrix products, arithmetic and copies ran while one was open for 1% of the time, Pallas kernels for 0%

commit v1 on v0

v1 whole, which is shorter than its diff:
```python
import jax
import jax.numpy as jnp
from jax import lax
from jax.experimental import pallas as pl
from jax.experimental.pallas import tpu as pltpu
from jax.sharding import PartitionSpec as P

FSWEEPS = 2
LSWEEPS = 3
USWEEPS = 3
MESH = pl.DeviceIdType.MESH
F32 = jnp.float32
BF16 = jnp.bfloat16
NN = (((1,), (0,)), ((), ()))
NT = (((1,), (1,)), ((), ()))


def split(x):
    hi = x.astype(BF16)
    lo = (x - hi.astype(F32)).astype(BF16)
    return hi, lo


def dot3(a, b, dims=NN):
    def one(p, q):
        return lax.dot_general(p, q, dims, preferred_element_type=F32)

    return one(a[0], b[0]) + (one(a[0], b[1]) + one(a[1], b[0]))


def make_kernel(n_dom, n_tile, rb, kd, blk, vecs, cap):
    own = rb // n_tile
    half = blk // 2
    slots = rb * kd
    sweeps = LSWEEPS + USWEEPS

    def kernel(
        kind, link, sends, kry, diag, inv, coup, inv_out, app_out,
        low_hi, low_lo, upp_hi, upp_lo, xall, out_q, part, fwd, pacc, ring_in, near_in2,
        vout, vpart, vrs, vfin, yown, send_sem, recv_sem, *tables,
    ):
        q_here, tables = tables[:FSWEEPS], tables[FSWEEPS:]
        q_there, tables = tables[:FSWEEPS], tables[FSWEEPS:]
        v_here, v_there = tables[:sweeps], tables[sweeps:]
        dom = lax.axis_index("dom")
        tile = lax.axis_index("tile")
        plus = {"tile": lax.rem(tile + 1, n_tile)}
        minus = {"tile": lax.rem(tile + n_tile - 1, n_tile)}
        doms = {d: {"dom": lax.rem(dom + n_dom + d, n_dom)} for d in (-2, -1, 1, 2)}

        barrier = pltpu.get_barrier_semaphore()
        peers = [{"tile": lax.rem(tile + d, n_tile)} for d in range(1, n_tile)]
        greeted = peers + list(doms.values())
        for dev in greeted:
            pl.semaphore_signal(barrier, inc=1, device_id=dev, device_id_type=MESH)
        pl.semaphore_wait(barrier, len(greeted))

        pending = []
        count = [0]

        def send(src, dst, dev):
            c = count[0]
            count[0] += 1
            copy = pltpu.make_async_remote_copy(
                src_ref=src, dst_ref=dst, send_sem=send_sem.at[c], recv_sem=recv_sem.at[c],
                device_id=dev, device_id_type=MESH,
            )
            copy.start()
            pending.append(copy)
            return copy

        def found(here, there, v, width):
            near = here[jnp.minimum(v, slots - 1) // width]
            remote = there[jnp.maximum(v - slots, 0)]
            return jnp.where(v < slots, near, remote)

        mine = pl.ds(tile * own, own)

        def gather_start(src, f):
            dst = xall.at[f]
            return (
                send(src.at[:, pl.ds(0, half)], dst.at[mine, pl.ds(0, half)], plus),
                send(src.at[:, pl.ds(half, half)], dst.at[mine, pl.ds(half, half)], minus),
                send(src.at[:, pl.ds(half, half)], dst.at[mine, pl.ds(half, half)], plus),
                send(src.at[:, pl.ds(0, half)], dst.at[mine, pl.ds(0, half)], minus),
            )

        def gather_finish(copies, f):
            dst = xall.at[f]
            left = pl.ds(lax.rem(tile + n_tile - 1, n_tile) * own, own)
            right = pl.ds(lax.rem(tile + 1, n_tile) * own, own)
            copies[0].wait_recv()
            a = dst.at[left, pl.ds(0, half)]
            more = send(a, a, plus)
            copies[1].wait_recv()
            b = dst.at[right, pl.ds(half, half)]
            more2 = send(b, b, minus)
            copies[2].wait_recv()
            copies[3].wait_recv()
            more.wait_recv()
            more2.wait_recv()

        first = gather_start(inv, 0)
        xall[0, mine] = inv[...]

        def prepare(r, _):
            for w in range(kd):
                cols = slice(w * blk, (w + 1) * blk)
                hi, lo = split(coup[r, w])
                zero = jnp.zeros_like(hi)
                k = kind[r, w]
                low_hi[r, :, cols] = jnp.where(k == 1, hi, zero)
                low_lo[r, :, cols] = jnp.where(k == 1, lo, zero)
                upp_hi[r, :, cols] = jnp.where(k == 2, hi, zero)
                upp_lo[r, :, cols] = jnp.where(k == 2, lo, zero)
            return _

        lax.fori_loop(0, rb, prepare, 0)
        gather_finish(first, 0)

        newest = inv
        for f in range(FSWEEPS):
            table, arrived = q_here[f], q_there[f]

            def upper(r, _):
                q = dot3(split(xall[f, r]), (upp_hi[r], upp_lo[r]))
                for w in range(kd):
                    table[r * kd + w] = q[:, w * blk : (w + 1) * blk]
                return _

            lax.fori_loop(0, rb, upper, 0, unroll=2)
            for l in range(2):
                for j in range(cap):
                    out_q[f, l * cap + j] = table[sends[l, j]]
            coming = [
                send(
                    out_q.at[f, pl.ds(l * cap, cap)],
                    arrived.at[pl.ds(l * cap, cap)],
                    doms[l + 1],
                )
                for l in range(2)
            ]
            for copy in coming:
                copy.wait_recv()

            def lower(r, _):
                q = jnp.concatenate([found(table, arrived, link[r, w], 1) for w in range(kd)], 0)
                part[f, r] = dot3((low_hi[r], low_lo[r]), split(q))
                return _

            lax.fori_loop(0, rb, lower, 0, unroll=2)

            far = pl.ds(lax.rem(tile + 2, n_tile) * own, own)
            right = pl.ds(lax.rem(tile + 1, n_tile) * own, own)
            left = pl.ds(lax.rem(tile + n_tile - 1, n_tile) * own, own)
            low_h, high_h = pl.ds(0, half), pl.ds(half, half)
            p = part.at[f]
            a = send(p.at[far, low_h], ring_in.at[f, 0], plus)
            b = send(p.at[far, high_h], ring_in.at[f, 1], minus)
            c = send(p.at[right, high_h], near_in2.at[f, 0, :, high_h], plus)
            d = send(p.at[left, low_h], near_in2.at[f, 1, :, low_h], minus)
            a.wait_recv()
            fwd[f, 0] = p[right, low_h] + ring_in[f, 0]
            e = send(fwd.at[f, 0], near_in2.at[f, 0, :, low_h], plus)
            b.wait_recv()
            fwd[f, 1] = p[left, high_h] + ring_in[f, 1]
            g = send(fwd.at[f, 1], near_in2.at[f, 1, :, high_h], minus)
            for copy in (c, d, e, g):
                copy.wait_recv()
            base = newest
            target = pacc.at[f]
            for i in range(own):
                pivot = diag[i] - (part[f, tile * own + i] + near_in2[f, 0, i] + near_in2[f, 1, i])
                x = base[i]
                xs = split(x)
                product = dot3(xs, split(pivot))
                target[i] = 2.0 * x - dot3(split(product), xs)
            newest = target
            if f < FSWEEPS - 1:
                copies = gather_start(target, f + 1)
                xall[f + 1, mine] = target[...]
                gather_finish(copies, f + 1)
        inv_out[...] = newest[...]

        def scaled(i, value):
            return dot3(split(value), split(newest[i]), NT)

        def spread_rows(dst):
            rows = dst.at[mine]
            copies = [send(rows, rows, peers[d]) for d in (1, 0, 2)]
            for copy in copies:
                copy.wait_recv()

        for i in range(own):
            v_here[0][tile * own + i] = scaled(i, kry[tile * own + i])
        for k in range(sweeps):
            lowering = k < LSWEEPS
            table, arrived = v_here[k], v_there[k]
            spread_rows(table)
            for l in range(2):
                for j in range(cap):
                    vout[k, l * cap + j] = table[sends[l + (0 if lowering else 2), j] // kd]
            sign = 1 if lowering else -1
            coming = [
                send(
                    vout.at[k, pl.ds(l * cap, cap)],
                    arrived.at[pl.ds(l * cap, cap)],
                    doms[sign * (l + 1)],
                )
                for l in range(2)
            ]
            for copy in coming:
                copy.wait_recv()
            hi_t, lo_t = (low_hi, low_lo) if lowering else (upp_hi, upp_lo)

            def products(r, _):
                v2 = jnp.concatenate([found(table, arrived, link[r, w], kd) for w in range(kd)], 1)
                vpart[k, r] = dot3(split(v2), (hi_t[r], lo_t[r]), NT)
                return _

            lax.fori_loop(0, rb, products, 0, unroll=3)
            copies = []
            for d in (1, 0, 2):
                rows = pl.ds(lax.rem(tile + d + 1, n_tile) * own, own)
                copies.append(send(vpart.at[k, rows], vrs.at[k, d], peers[d]))
            for copy in copies:
                copy.wait_recv()
            for i in range(own):
                total = vpart[k, tile * own + i] + vrs[k, 0, i] + vrs[k, 1, i] + vrs[k, 2, i]
                if lowering:
                    y = kry[tile * own + i] - total
                    if k == LSWEEPS - 1:
                        yown[i] = y
                    value = y
                else:
                    value = yown[i] - total
                result = scaled(i, value)
                if k < sweeps - 1:
                    v_here[k + 1][tile * own + i] = result
                else:
                    vfin[tile * own + i] = result
        spread_rows(vfin)
        app_out[...] = vfin[...]
        for copy in pending:
            copy.wait_send()

    return kernel


def solution(mesh):
    n_dom, n_tile = mesh.shape["dom"], mesh.shape["tile"]

    def local(krylov_block, diag_block, inverse_prev, coupling_tiles, slot_kind, slot_link, send_slots):
        rb, vecs, blk = krylov_block.shape
        kd = coupling_tiles.shape[1]
        cap = send_slots.shape[3]
        own = rb // n_tile
        slots = rb * kd
        sweeps = LSWEEPS + USWEEPS
        n_copies = FSWEEPS * (6 + 2 + 6) + sweeps * 8 + 3
        vm = pl.BlockSpec(memory_space=pltpu.VMEM)
        sm = pl.BlockSpec(memory_space=pltpu.SMEM)
        return pl.pallas_call(
            make_kernel(n_dom, n_tile, rb, kd, blk, vecs, cap),
            out_shape=(
                jax.ShapeDtypeStruct((own, blk, blk), F32),
                jax.ShapeDtypeStruct((rb, vecs, blk), F32),
            ),
            in_specs=[sm] * 3 + [vm] * 4,
            out_specs=(vm, vm),
            scratch_shapes=[
                pltpu.VMEM((rb, blk, kd * blk), BF16),
                pltpu.VMEM((rb, blk, kd * blk), BF16),
                pltpu.VMEM((rb, blk, kd * blk), BF16),
                pltpu.VMEM((rb, blk, kd * blk), BF16),
                pltpu.VMEM((FSWEEPS, rb, blk, blk), F32),
                pltpu.VMEM((FSWEEPS, 2 * cap, blk, blk), F32),
                pltpu.VMEM((FSWEEPS, rb, blk, blk), F32),
                pltpu.VMEM((FSWEEPS, 2, own, blk // 2, blk), F32),
                pltpu.VMEM((FSWEEPS, own, blk, blk), F32),
                pltpu.VMEM((FSWEEPS, 2, own, blk // 2, blk), F32),
                pltpu.VMEM((FSWEEPS, 2, own, blk, blk), F32),
                pltpu.VMEM((sweeps, 2 * cap, vecs, blk), F32),
                pltpu.VMEM((sweeps, rb, vecs, blk), F32),
                pltpu.VMEM((sweeps, n_tile - 1, own, vecs, blk), F32),
                pltpu.VMEM((rb, vecs, blk), F32),
                pltpu.VMEM((own, vecs, blk), F32),
                pltpu.SemaphoreType.DMA((n_copies,)),
                pltpu.SemaphoreType.DMA((n_copies,)),
            ]
            + [pltpu.VMEM((slots, blk, blk), F32)] * FSWEEPS
            + [pltpu.VMEM((2 * cap, blk, blk), F32)] * FSWEEPS
            + [pltpu.VMEM((rb, vecs, blk), F32)] * sweeps
            + [pltpu.VMEM((2 * cap, vecs, blk), F32)] * sweeps,
            compiler_params=pltpu.CompilerParams(
                collective_id=0, has_side_effects=True, vmem_limit_bytes=48 * 1024 * 1024
            ),
        )(
            slot_kind, slot_link, send_slots.reshape(4, cap),
            krylov_block, diag_block, inverse_prev, coupling_tiles,
        )

    placed = (
        P("dom", None, None),
        P(("dom", "tile"), None, None),
        P(("dom", "tile"), None, None),
        P("dom", "tile", None, None),
        P("dom", "tile"),
        P("dom", "tile"),
        P("dom", "tile", None, None),
    )
    return jax.shard_map(
        local,
        mesh=mesh,
        in_specs=placed,
        out_specs=(P(("dom", "tile"), None, None), P("dom", None, None)),
        check_vma=False,
    )
```

time: 331 us -> 173 us (0.52)
  the two profiles are of different devices: /device:TPU:230 before, /device:TPU:2 now
where the time goes in v1:
time: 173 us
  Pallas kernels  165 us (95%)
  local copies, waits for them, and re-layouts  7.76 us (4%)
    pallas_call x1, Pallas kernels, local(): pl.pallas_call(make_kernel(n_dom, n_tile, rb, kd, blk, vecs, cap), out_sh...  165 us
    unnamed x14, local copies, waits for them, and re-layouts  7.76 us

profile of v1, /device:TPU:2, one launch (start us, length us, event | category | flops | bytes accessed | tf_op | source)
XLA Modules:
  0.0 172.9 jit_solution(3214997936919022510)
XLA Ops:
  0.6 0.8 copy.9.kind
  1.4 0.8 copy.10.link
  2.2 0.0 copy-start
  2.2 1.4 copy-done
  3.6 0.0 copy-start.1
  3.6 0.9 copy-done.1
  4.5 0.0 copy-start.2
  4.5 0.9 copy-done.2
  5.4 0.0 copy-start.3
  5.4 0.9 copy-done.3
  6.4 0.0 copy-start.4
  6.4 0.7 copy-done.4
  7.0 164.5 %shard_map.86 = (f32[3,128,128]{2,1,0:T(8,128)S(1)}, f32[12,32,128]{2,1,0:T(8,128)S(1)}) custom-call(s32[12,2]{1,0:T(8,128)S(1)} %copy.9.kind, s32[12,2]{1,0:T(8,128)S(1)} %copy.10.link, s32[4,4]{1,0:T(4,128)S(1)} %bitcast.1, f32[12,32,128]{2,1,0:T(8,128)S(1)} %copy-done.1, f32[3,128,128]{2,1,0:T(8,128)S(1)} %copy-done.2, f32[3,128,128]{2,1,0:T(8,128)S(1)} %copy-done.3, ...), custom_call_target="tpu_custom_call" | custom-call | tf_op jit(solution)/shard_map/pallas_call | solution.py:263
  171.6 0.7 copy.13
  172.3 0.7 copy.14
Async XLA Ops:
  2.2 1.4 copy-start
  3.6 0.9 copy-start.1
  4.5 0.9 copy-start.2
  5.4 0.9 copy-start.3
  6.4 0.7 copy-start.4

commit v2 on v1

v2 whole, which is shorter than its diff:
```python
import jax
import jax.numpy as jnp
from jax import lax
from jax.experimental import pallas as pl
from jax.experimental.pallas import tpu as pltpu
from jax.sharding import PartitionSpec as P

FSWEEPS = 2
LSWEEPS = 3
USWEEPS = 3
CHUNKS = 2
HALVES = 2
ROWS = 3
MESH = pl.DeviceIdType.MESH
F32 = jnp.float32
BF16 = jnp.bfloat16
NN = (((1,), (0,)), ((), ()))
NT = (((1,), (1,)), ((), ()))


def split(x):
    hi = x.astype(BF16)
    lo = (x - hi.astype(F32)).astype(BF16)
    return hi, lo


def dot3(a, b, dims=NN):
    def one(p, q):
        return lax.dot_general(p, q, dims, preferred_element_type=F32)

    return one(a[0], b[0]) + (one(a[0], b[1]) + one(a[1], b[0]))


def make_kernel(n_dom, n_tile, rb, kd, blk, vecs, cap):
    own = rb // n_tile
    slots = rb * kd
    sweeps = LSWEEPS + USWEEPS
    vc = vecs // CHUNKS
    part_rows = blk // HALVES
    piece = part_rows // 2
    half = blk // 2

    def kernel(
        kind_in, link_in, sends_in, kry_in, diag_in, inv_in, coup_in, inv_out, app_out,
        kind, link, sends, kry, diag, inv, coup, load_sem,
        low_hi, low_lo, upp_hi, upp_lo, xall, out_q, part, fwd, pacc, ring_in, near_in2, x_hi, x_lo,
        vout, vpart, vrs, vfin, yown, send_sem, recv_sem, *tables,
    ):
        q_here, tables = tables[:FSWEEPS], tables[FSWEEPS:]
        q_there, tables = tables[:FSWEEPS], tables[FSWEEPS:]
        v_here, v_there = tables[: sweeps * CHUNKS], tables[sweeps * CHUNKS :]

        sources = (inv_in, coup_in, sends_in, link_in, kind_in, diag_in, kry_in)
        targets = (inv, coup, sends, link, kind, diag, kry)
        loads = [
            pltpu.make_async_copy(a, b, load_sem.at[i]) for i, (a, b) in enumerate(zip(sources, targets))
        ]
        for load in loads:
            load.start()

        dom = lax.axis_index("dom")
        tile = lax.axis_index("tile")
        plus = {"tile": lax.rem(tile + 1, n_tile)}
        minus = {"tile": lax.rem(tile + n_tile - 1, n_tile)}
        doms = {d: {"dom": lax.rem(dom + n_dom + d, n_dom)} for d in (-2, -1, 1, 2)}

        barrier = pltpu.get_barrier_semaphore()
        peers = [{"tile": lax.rem(tile + d, n_tile)} for d in range(1, n_tile)]
        greeted = peers + list(doms.values())
        for dev in greeted:
            pl.semaphore_signal(barrier, inc=1, device_id=dev, device_id_type=MESH)
        loads[0].wait()
        pl.semaphore_wait(barrier, len(greeted))

        pending = []
        count = [0]

        def send(src, dst, dev):
            c = count[0]
            count[0] += 1
            copy = pltpu.make_async_remote_copy(
                src_ref=src, dst_ref=dst, send_sem=send_sem.at[c], recv_sem=recv_sem.at[c],
                device_id=dev, device_id_type=MESH,
            )
            copy.start()
            pending.append(copy)
            return copy

        def found(here, there, v, width, *rest):
            near = here[(jnp.minimum(v, slots - 1) // width, *rest)]
            remote = there[(jnp.maximum(v - slots, 0), *rest)]
            return jnp.where(v < slots, near, remote)

        def group(d):
            return lax.rem(tile + d, n_tile) * own

        mine, right, far, left = (pl.ds(group(d), own) for d in range(n_tile))

        class Gather:
            def __init__(self, src, f):
                self.src, self.dst, self.copies = src, xall.at[f], {}

            def cut(self, c, p):
                return pl.ds(c * part_rows + p * piece, piece)

            def out(self, c, p, dev):
                rows = self.cut(c, p)
                self.copies[c, p, dev is plus] = send(self.src.at[:, rows], self.dst.at[mine, rows], dev)

            def first(self, c):
                self.out(c, 0, plus)
                self.out(c, 1, minus)

            def second(self, c):
                self.out(c, 1, plus)
                self.out(c, 0, minus)

            def relay(self, c):
                for p, rows, dev in ((0, left, plus), (1, right, minus)):
                    self.copies[c, p, dev is plus].wait_recv()
                    block = self.dst.at[rows, self.cut(c, p)]
                    self.copies[c, p] = send(block, block, dev)

            def done(self, c):
                self.copies[c, 1, True].wait_recv()
                self.copies[c, 0, False].wait_recv()
                self.copies[c, 0].wait_recv()
                self.copies[c, 1].wait_recv()

        def prepare(r, _):
            for w in range(kd):
                cols = slice(w * blk, (w + 1) * blk)
                hi, lo = split(coup[r, w])
                zero = jnp.zeros_like(hi)
                k = kind[w, r]
                low_hi[r, :, cols] = jnp.where(k == 1, hi, zero)
                low_lo[r, :, cols] = jnp.where(k == 1, lo, zero)
                upp_hi[r, :, cols] = jnp.where(k == 2, hi, zero)
                upp_lo[r, :, cols] = jnp.where(k == 2, lo, zero)
            return _

        gather = Gather(inv, 0)
        for c in range(HALVES):
            gather.first(c)
            if c == 0:
                gather.second(c)
        xall[0, mine] = inv[...]

        newest = inv
        for f in range(FSWEEPS):
            table, arrived = q_here[f], q_there[f]
            gather.relay(0)
            for c in range(1, HALVES):
                gather.second(c)
            if f == 0:
                for load in loads[1:]:
                    load.wait()
                lax.fori_loop(0, rb, prepare, 0)
            coming = []
            for c in range(HALVES):
                gather.done(c)
                if c + 1 < HALVES:
                    gather.relay(c + 1)
                rows = pl.ds(c * part_rows, part_rows)

                def upper(r, _):
                    q = dot3(split(xall[f, r, rows]), (upp_hi[r], upp_lo[r]))
                    for w in range(kd):
                        table[r * kd + w, rows] = q[:, w * blk : (w + 1) * blk]
                    return _

                lax.fori_loop(0, rb, upper, 0, unroll=3)
                for l in (1, 0):
                    for j in range(cap):
                        out_q[f, l * cap + j, rows] = table[sends[l, j], rows]
                    cut = pl.ds(l * cap, cap)
                    coming.append(send(out_q.at[f, cut, rows], arrived.at[cut, rows], doms[l + 1]))
            for copy in coming:
                copy.wait_recv()

            def lower(base):
                for i in range(own):
                    r = base + i
                    q = jnp.concatenate([found(table, arrived, link[w, r], 1) for w in range(kd)], 0)
                    part[f, r] = dot3((low_hi[r], low_lo[r]), split(q))

            low_h, high_h = pl.ds(0, half), pl.ds(half, half)
            p = part.at[f]
            lower(group(2))
            a = send(p.at[far, low_h], ring_in.at[f, 0], plus)
            b = send(p.at[far, high_h], ring_in.at[f, 1], minus)
            lower(group(1))
            c = send(p.at[right, high_h], near_in2.at[f, 0, :, high_h], plus)
            lower(group(3))
            d = send(p.at[left, low_h], near_in2.at[f, 1, :, low_h], minus)
            a.wait_recv()
            fwd[f, 0] = p[right, low_h] + ring_in[f, 0]
            e = send(fwd.at[f, 0], near_in2.at[f, 0, :, low_h], plus)
            b.wait_recv()
            fwd[f, 1] = p[left, high_h] + ring_in[f, 1]
            g = send(fwd.at[f, 1], near_in2.at[f, 1, :, high_h], minus)
            lower(group(0))
            for copy in (c, d, e, g):
                copy.wait_recv()
            base = newest
            target = pacc.at[f]
            last = f == FSWEEPS - 1
            for i in range(own):
                pivot = diag[i] - (part[f, tile * own + i] + near_in2[f, 0, i] + near_in2[f, 1, i])
                x = base[i]
                xs = split(x)
                product = dot3(xs, split(pivot))
                fresh = 2.0 * x - dot3(split(product), xs)
                target[i] = fresh
                if last:
                    x_hi[i], x_lo[i] = split(fresh)
                else:
                    xall[f + 1, tile * own + i] = fresh
            newest = target
            if not last:
                gather = Gather(target, f + 1)
                for c in range(HALVES):
                    gather.first(c)
                    if c == 0:
                        gather.second(c)

        def scaled(i, value):
            return dot3(split(value), (x_hi[i], x_lo[i]), NT)

        def spread_rows(dst):
            rows = dst.at[mine]
            return [send(rows, rows, peers[d]) for d in (1, 0, 2)]

        def kry_rows(i, c):
            return kry[tile * own + i, c * vc : (c + 1) * vc]

        spreading = {}
        for c in range(CHUNKS):
            for i in range(own):
                v_here[c][tile * own + i] = scaled(i, kry_rows(i, c))
            spreading[c] = spread_rows(v_here[c])
        stores = [pltpu.make_async_copy(newest, inv_out, load_sem.at[0])]
        stores[0].start()
        for k in range(sweeps):
            lowering = k < LSWEEPS
            hi_t, lo_t = (low_hi, low_lo) if lowering else (upp_hi, upp_lo)
            sign = 1 if lowering else -1
            moving, summing = {}, {}
            for c in range(CHUNKS):
                table, arrived = v_here[k * CHUNKS + c], v_there[k * CHUNKS + c]
                for copy in spreading[c]:
                    copy.wait_recv()
                moving[c] = []
                for l in (1, 0):
                    for j in range(cap):
                        vout[k, c, l * cap + j] = table[sends[l + (0 if lowering else 2), j] // kd]
                    cut = pl.ds(l * cap, cap)
                    moving[c].append(send(vout.at[k, c, cut], arrived.at[cut], doms[sign * (l + 1)]))
            for c in range(CHUNKS):
                table, arrived = v_here[k * CHUNKS + c], v_there[k * CHUNKS + c]
                for copy in moving[c]:
                    copy.wait_recv()

                def products(r, _):
                    v2 = jnp.concatenate([found(table, arrived, link[w, r], kd) for w in range(kd)], 1)
                    vpart[k, c, r] = dot3(split(v2), (hi_t[r], lo_t[r]), NT)
                    return _

                lax.fori_loop(0, rb, products, 0, unroll=ROWS)
                summing[c] = []
                for d in (1, 0, 2):
                    rows = pl.ds(group(d + 1), own)
                    summing[c].append(send(vpart.at[k, c, rows], vrs.at[k, c, d], peers[d]))
            for c in range(CHUNKS):
                for copy in summing[c]:
                    copy.wait_recv()
                for i in range(own):
                    total = (
                        vpart[k, c, tile * own + i] + vrs[k, c, 0, i] + vrs[k, c, 1, i] + vrs[k, c, 2, i]
                    )
                    if lowering:
                        value = kry_rows(i, c) - total
                        if k == LSWEEPS - 1:
                            yown[c, i] = value
                    else:
                        value = yown[c, i] - total
                    result = scaled(i, value)
                    if k < sweeps - 1:
                        v_here[(k + 1) * CHUNKS + c][tile * own + i] = result
                    else:
                        vfin[c, tile * own + i] = result
                spreading[c] = spread_rows(v_here[(k + 1) * CHUNKS + c] if k < sweeps - 1 else vfin.at[c])
        for c in range(CHUNKS):
            for copy in spreading[c]:
                copy.wait_recv()
            stores.append(pltpu.make_async_copy(vfin.at[c], app_out.at[:, pl.ds(c * vc, vc)], load_sem.at[c + 1]))
            stores[-1].start()
        for copy in pending:
            copy.wait_send()
        for store in stores:
            store.wait()

    return kernel


def solution(mesh):
    n_dom, n_tile = mesh.shape["dom"], mesh.shape["tile"]

    def local(krylov_block, diag_block, inverse_prev, coupling_tiles, slot_kind, slot_link, send_slots):
        rb, vecs, blk = krylov_block.shape
        kd = coupling_tiles.shape[1]
        cap = send_slots.shape[3]
        own = rb // n_tile
        slots = rb * kd
        sweeps = LSWEEPS + USWEEPS
        vc = vecs // CHUNKS
        n_copies = FSWEEPS * (6 * HALVES + 2 * HALVES + 6) + CHUNKS * (sweeps * 8 + 3)
        hbm = pl.BlockSpec(memory_space=pltpu.HBM)
        return pl.pallas_call(
            make_kernel(n_dom, n_tile, rb, kd, blk, vecs, cap),
            out_shape=(
                jax.ShapeDtypeStruct((own, blk, blk), F32),
                jax.ShapeDtypeStruct((rb, vecs, blk), F32),
            ),
            in_specs=[hbm] * 7,
            out_specs=(hbm, hbm),
            scratch_shapes=[
                pltpu.SMEM((kd, rb), jnp.int32),
                pltpu.SMEM((kd, rb), jnp.int32),
                pltpu.SMEM((4, cap), jnp.int32),
                pltpu.VMEM((rb, vecs, blk), F32),
                pltpu.VMEM((own, blk, blk), F32),
                pltpu.VMEM((own, blk, blk), F32),
                pltpu.VMEM((rb, kd, blk, blk), F32),
                pltpu.SemaphoreType.DMA((7,)),
                pltpu.VMEM((rb, blk, kd * blk), BF16),
                pltpu.VMEM((rb, blk, kd * blk), BF16),
                pltpu.VMEM((rb, blk, kd * blk), BF16),
                pltpu.VMEM((rb, blk, kd * blk), BF16),
                pltpu.VMEM((FSWEEPS, rb, blk, blk), F32),
                pltpu.VMEM((FSWEEPS, 2 * cap, blk, blk), F32),
                pltpu.VMEM((FSWEEPS, rb, blk, blk), F32),
                pltpu.VMEM((FSWEEPS, 2, own, blk // 2, blk), F32),
                pltpu.VMEM((FSWEEPS, own, blk, blk), F32),
                pltpu.VMEM((FSWEEPS, 2, own, blk // 2, blk), F32),
                pltpu.VMEM((FSWEEPS, 2, own, blk, blk), F32),
                pltpu.VMEM((own, blk, blk), BF16),
                pltpu.VMEM((own, blk, blk), BF16),
                pltpu.VMEM((sweeps, CHUNKS, 2 * cap, vc, blk), F32),
                pltpu.VMEM((sweeps, CHUNKS, rb, vc, blk), F32),
                pltpu.VMEM((sweeps, CHUNKS, n_tile - 1, own, vc, blk), F32),
                pltpu.VMEM((CHUNKS, rb, vc, blk), F32),
                pltpu.VMEM((CHUNKS, own, vc, blk), F32),
                pltpu.SemaphoreType.DMA((n_copies,)),
                pltpu.SemaphoreType.DMA((n_copies,)),
            ]
            + [pltpu.VMEM((slots, blk, blk), F32)] * FSWEEPS
            + [pltpu.VMEM((2 * cap, blk, blk), F32)] * FSWEEPS
            + [pltpu.VMEM((rb, vc, blk), F32)] * (sweeps * CHUNKS)
            + [pltpu.VMEM((2 * cap, vc, blk), F32)] * (sweeps * CHUNKS),
            compiler_params=pltpu.CompilerParams(
                collective_id=0, has_side_effects=True, vmem_limit_bytes=66_600_000
            ),
        )(
            slot_kind.T, slot_link.T, send_slots.reshape(4, cap),
            krylov_block, diag_block, inverse_prev, coupling_tiles,
        )

    placed = (
        P("dom", None, None),
        P(("dom", "tile"), None, None),
        P(("dom", "tile"), None, None),
        P("dom", "tile", None, None),
        P("dom", "tile"),
        P("dom", "tile"),
        P("dom", "tile", None, None),
    )
    return jax.shard_map(
        local,
        mesh=mesh,
        in_specs=placed,
        out_specs=(P(("dom", "tile"), None, None), P("dom", None, None)),
        check_vma=False,
    )
```

time: 173 us -> 151 us (0.87)
  Pallas kernels: 165 us -> 147 us
  local copies, waits for them, and re-layouts: 7.76 us -> 3.23 us
    pallas_call x1, Pallas kernels: 165 us -> 147 us  [local(): pl.pallas_call(make_kernel(n_dom, n_tile, rb, kd, blk, vecs, cap), out_sh...]
    unnamed x14 -> x2, local copies, waits for them, and re-layouts: 7.76 us -> 3.23 us
where the time goes in v2:
time: 151 us
  Pallas kernels  147 us (97%)
  local copies, waits for them, and re-layouts  3.23 us (2%)
    pallas_call x1, Pallas kernels, local(): pl.pallas_call(make_kernel(n_dom, n_tile, rb, kd, blk, vecs, cap), out_sh...  147 us
    unnamed x2, local copies, waits for them, and re-layouts  3.23 us

profile of v2, /device:TPU:2, one launch (start us, length us, event | category | flops | bytes accessed | tf_op | source)
XLA Modules:
  0.0 151.2 jit_solution(6196846236835674284)
XLA Ops:
  0.6 147.4 %shard_map.86 = (f32[3,128,128]{2,1,0:T(8,128)}, f32[12,32,128]{2,1,0:T(8,128)}) custom-call(s32[2,12]{1,0:T(2,128)} %bitcast.4, s32[2,12]{1,0:T(2,128)} %bitcast.5, s32[4,4]{1,0:T(4,128)} %bitcast.3, f32[12,32,128]{2,1,0:T(8,128)} %kry_in.1, f32[3,128,128]{2,1,0:T(8,128)} %diag_in.1, f32[3,128,128]{2,1,0:T(8,128)} %inv_in.1, f32[12,2,128,128]{3,2,1,0:T(8,128)} %coup_in.1), custom_call_target="tpu_custom_call" | custom-call | tf_op jit(solution)/shard_map/pallas_call | solution.py:319
  148.0 1.6 %copy.11 = f32[3,128,128]{2,1,0:T(8,128)} copy(f32[3,128,128]{2,1,0:T(8,128)} %get-tuple-element.4) | data formatting | bytes 393216
  149.6 1.6 %copy.12 = f32[12,32,128]{2,1,0:T(8,128)} copy(f32[12,32,128]{2,1,0:T(8,128)} %get-tuple-element.5) | data formatting | bytes 393216

commit v3 on v2

--- a/solution.py
+++ b/solution.py
@@ -28,7 +28,9 @@
     def one(p, q):
         return lax.dot_general(p, q, dims, preferred_element_type=F32)
 
-    return one(a[0], b[0]) + (one(a[0], b[1]) + one(a[1], b[0]))
+    rows = a[0].shape[0]
+    both = one(jnp.concatenate(a, 0), b[0])
+    return both[:rows] + (one(a[0], b[1]) + both[rows:])
 
 
 def make_kernel(n_dom, n_tile, rb, kd, blk, vecs, cap):
@@ -107,19 +109,20 @@
                 rows = self.cut(c, p)
                 self.copies[c, p, dev is plus] = send(self.src.at[:, rows], self.dst.at[mine, rows], dev)
 
-            def first(self, c):
-                self.out(c, 0, plus)
-                self.out(c, 1, minus)
-
-            def second(self, c):
-                self.out(c, 1, plus)
-                self.out(c, 0, minus)
+            def lead(self, c):
+                if 0 < c <= HALVES:
+                    self.out(c - 1, 1, plus)
+                    self.out(c - 1, 0, minus)
+                if c < HALVES:
+                    self.out(c, 0, plus)
+                    self.out(c, 1, minus)
 
             def relay(self, c):
                 for p, rows, dev in ((0, left, plus), (1, right, minus)):
                     self.copies[c, p, dev is plus].wait_recv()
                     block = self.dst.at[rows, self.cut(c, p)]
                     self.copies[c, p] = send(block, block, dev)
+                self.lead(c + 2)
 
             def done(self, c):
                 self.copies[c, 1, True].wait_recv()
@@ -140,18 +143,14 @@
             return _
 
         gather = Gather(inv, 0)
-        for c in range(HALVES):
-            gather.first(c)
-            if c == 0:
-                gather.second(c)
+        gather.lead(0)
+        gather.lead(1)
         xall[0, mine] = inv[...]
 
         newest = inv
         for f in range(FSWEEPS):
             table, arrived = q_here[f], q_there[f]
             gather.relay(0)
-            for c in range(1, HALVES):
-                gather.second(c)
             if f == 0:
                 for load in loads[1:]:
                     load.wait()
@@ -205,24 +204,25 @@
             base = newest
             target = pacc.at[f]
             last = f == FSWEEPS - 1
+            pivots = []
             for i in range(own):
                 pivot = diag[i] - (part[f, tile * own + i] + near_in2[f, 0, i] + near_in2[f, 1, i])
-                x = base[i]
-                xs = split(x)
-                product = dot3(xs, split(pivot))
-                fresh = 2.0 * x - dot3(split(product), xs)
-                target[i] = fresh
-                if last:
-                    x_hi[i], x_lo[i] = split(fresh)
-                else:
-                    xall[f + 1, tile * own + i] = fresh
+                pivots.append((split(pivot), split(base[i])))
+            gather = None if last else Gather(target, f + 1)
+            cuts = [pl.ds(0, blk)] if last else [pl.ds(0, half), pl.ds(half, half)]
+            for h, rows in enumerate(cuts):
+                for i in range(own):
+                    x = base[i, rows]
+                    product = dot3(split(x), pivots[i][0])
+                    fresh = 2.0 * x - dot3(split(product), pivots[i][1])
+                    target[i, rows] = fresh
+                    if last:
+                        x_hi[i], x_lo[i] = split(fresh)
+                    else:
+                        xall[f + 1, tile * own + i, rows] = fresh
+                if not last:
+                    gather.lead(h)
             newest = target
-            if not last:
-                gather = Gather(target, f + 1)
-                for c in range(HALVES):
-                    gather.first(c)
-                    if c == 0:
-                        gather.second(c)
 
         def scaled(i, value):
             return dot3(split(value), (x_hi[i], x_lo[i]), NT)
@@ -239,8 +239,7 @@
             for i in range(own):
                 v_here[c][tile * own + i] = scaled(i, kry_rows(i, c))
             spreading[c] = spread_rows(v_here[c])
-        stores = [pltpu.make_async_copy(newest, inv_out, load_sem.at[0])]
-        stores[0].start()
+        inv_out[...] = newest[...]
         for k in range(sweeps):
             lowering = k < LSWEEPS
             hi_t, lo_t = (low_hi, low_lo) if lowering else (upp_hi, upp_lo)
@@ -293,12 +292,9 @@
         for c in range(CHUNKS):
             for copy in spreading[c]:
                 copy.wait_recv()
-            stores.append(pltpu.make_async_copy(vfin.at[c], app_out.at[:, pl.ds(c * vc, vc)], load_sem.at[c + 1]))
-            stores[-1].start()
+            app_out[:, c * vc : (c + 1) * vc] = vfin[c]
         for copy in pending:
             copy.wait_send()
-        for store in stores:
-            store.wait()
 
     return kernel
 
@@ -315,6 +311,7 @@
         sweeps = LSWEEPS + USWEEPS
         vc = vecs // CHUNKS
         n_copies = FSWEEPS * (6 * HALVES + 2 * HALVES + 6) + CHUNKS * (sweeps * 8 + 3)
+        vm = pl.BlockSpec(memory_space=pltpu.VMEM)
         hbm = pl.BlockSpec(memory_space=pltpu.HBM)
         return pl.pallas_call(
             make_kernel(n_dom, n_tile, rb, kd, blk, vecs, cap),
@@ -323,7 +320,7 @@
                 jax.ShapeDtypeStruct((rb, vecs, blk), F32),
             ),
             in_specs=[hbm] * 7,
-            out_specs=(hbm, hbm),
+            out_specs=(vm, vm),
             scratch_shapes=[
                 pltpu.SMEM((kd, rb), jnp.int32),
                 pltpu.SMEM((kd, rb), jnp.int32),
@@ -359,11 +356,16 @@
             + [pltpu.VMEM((rb, vc, blk), F32)] * (sweeps * CHUNKS)
             + [pltpu.VMEM((2 * cap, vc, blk), F32)] * (sweeps * CHUNKS),
             compiler_params=pltpu.CompilerParams(
-                collective_id=0, has_side_effects=True, vmem_limit_bytes=66_600_000
+                collective_id=0, has_side_effects=True, vmem_limit_bytes=48 * 1024 * 1024
             ),
         )(
-            slot_kind.T, slot_link.T, send_slots.reshape(4, cap),
-            krylov_block, diag_block, inverse_prev, coupling_tiles,
+            *(
+                pltpu.with_memory_space_constraint(x, pltpu.HBM)
+                for x in (
+                    slot_kind.T, slot_link.T, send_slots.reshape(4, cap),
+                    krylov_block, diag_block, inverse_prev, coupling_tiles,
+                )
+            )
         )
 
     placed = (

time: 151 us -> 147 us (0.974)
  the two profiles are of different devices: /device:TPU:2 before, /device:TPU:1 now
where the time goes in v3:
time: 147 us
  Pallas kernels  145 us (99%)
    pallas_call x1, Pallas kernels, local(): pl.pallas_call(make_kernel(n_dom, n_tile, rb, kd, blk, vecs, cap), out_sh...  145 us

profile of v3, /device:TPU:1, one launch (start us, length us, event | category | flops | bytes accessed | tf_op | source)
XLA Modules:
  0.0 147.3 jit_solution(16116538574608433941)
XLA Ops:
  0.6 145.3 %shard_map.86 = (f32[3,128,128]{2,1,0:T(8,128)S(1)}, f32[12,32,128]{2,1,0:T(8,128)S(1)}) custom-call(s32[2,12]{1,0:T(2,128)} %bitcast.4, s32[2,12]{1,0:T(2,128)} %bitcast.5, s32[4,4]{1,0:T(4,128)} %bitcast.3, f32[12,32,128]{2,1,0:T(8,128)} %kry_in.1, f32[3,128,128]{2,1,0:T(8,128)} %diag_in.1, f32[3,128,128]{2,1,0:T(8,128)} %inv_in.1, f32[12,2,128,128]{3,2,1,0:T(8,128)} %coup_in.1), custom_call_target="tpu_custom_call" | custom-call | tf_op jit(solution)/shard_map/pallas_call | solution.py:316
  145.9 0.7 copy.11
  146.6 0.7 copy.12

commit v4 on v3

--- a/solution.py
+++ b/solution.py
@@ -8,9 +8,9 @@
 FSWEEPS = 2
 LSWEEPS = 3
 USWEEPS = 3
-CHUNKS = 2
+CHUNKS = 4
 HALVES = 2
-ROWS = 3
+ROWS = 12
 MESH = pl.DeviceIdType.MESH
 F32 = jnp.float32
 BF16 = jnp.bfloat16
@@ -45,7 +45,7 @@
     def kernel(
         kind_in, link_in, sends_in, kry_in, diag_in, inv_in, coup_in, inv_out, app_out,
         kind, link, sends, kry, diag, inv, coup, load_sem,
-        low_hi, low_lo, upp_hi, upp_lo, xall, out_q, part, fwd, pacc, ring_in, near_in2, x_hi, x_lo,
+        low_hi, low_lo, upp_hi, upp_lo, low_t_hi, low_t_lo, upp_t_hi, upp_t_lo, xall, out_q, part, fwd, pacc, ring_in, near_in2, x_hi, x_lo,
         vout, vpart, vrs, vfin, yown, send_sem, recv_sem, *tables,
     ):
         q_here, tables = tables[:FSWEEPS], tables[FSWEEPS:]
@@ -140,6 +140,18 @@
                 low_lo[r, :, cols] = jnp.where(k == 1, lo, zero)
                 upp_hi[r, :, cols] = jnp.where(k == 2, hi, zero)
                 upp_lo[r, :, cols] = jnp.where(k == 2, lo, zero)
+            return _
+
+        def flip(r, _):
+            for w in range(kd):
+                rows = slice(w * blk, (w + 1) * blk)
+                hi, lo = split(coup[r, w].T)
+                zero = jnp.zeros_like(hi)
+                k = kind[w, r]
+                low_t_hi[r, rows] = jnp.where(k == 1, hi, zero)
+                low_t_lo[r, rows] = jnp.where(k == 1, lo, zero)
+                upp_t_hi[r, rows] = jnp.where(k == 2, hi, zero)
+                upp_t_lo[r, rows] = jnp.where(k == 2, lo, zero)
             return _
 
         gather = Gather(inv, 0)
@@ -168,12 +180,14 @@
                         table[r * kd + w, rows] = q[:, w * blk : (w + 1) * blk]
                     return _
 
-                lax.fori_loop(0, rb, upper, 0, unroll=3)
+                lax.fori_loop(0, rb, upper, 0, unroll=6)
                 for l in (1, 0):
                     for j in range(cap):
                         out_q[f, l * cap + j, rows] = table[sends[l, j], rows]
                     cut = pl.ds(l * cap, cap)
                     coming.append(send(out_q.at[f, cut, rows], arrived.at[cut, rows], doms[l + 1]))
+            if f == 0:
+                lax.fori_loop(0, rb, flip, 0)
             for copy in coming:
                 copy.wait_recv()
 
@@ -242,7 +256,7 @@
         inv_out[...] = newest[...]
         for k in range(sweeps):
             lowering = k < LSWEEPS
-            hi_t, lo_t = (low_hi, low_lo) if lowering else (upp_hi, upp_lo)
+            hi_t, lo_t = (low_t_hi, low_t_lo) if lowering else (upp_t_hi, upp_t_lo)
             sign = 1 if lowering else -1
             moving, summing = {}, {}
             for c in range(CHUNKS):
@@ -262,7 +276,7 @@
 
                 def products(r, _):
                     v2 = jnp.concatenate([found(table, arrived, link[w, r], kd) for w in range(kd)], 1)
-                    vpart[k, c, r] = dot3(split(v2), (hi_t[r], lo_t[r]), NT)
+                    vpart[k, c, r] = dot3(split(v2), (hi_t[r], lo_t[r]))
                     return _
 
                 lax.fori_loop(0, rb, products, 0, unroll=ROWS)
@@ -334,6 +348,10 @@
                 pltpu.VMEM((rb, blk, kd * blk), BF16),
                 pltpu.VMEM((rb, blk, kd * blk), BF16),
                 pltpu.VMEM((rb, blk, kd * blk), BF16),
+                pltpu.VMEM((rb, kd * blk, blk), BF16),
+                pltpu.VMEM((rb, kd * blk, blk), BF16),
+                pltpu.VMEM((rb, kd * blk, blk), BF16),
+                pltpu.VMEM((rb, kd * blk, blk), BF16),
                 pltpu.VMEM((FSWEEPS, rb, blk, blk), F32),
                 pltpu.VMEM((FSWEEPS, 2 * cap, blk, blk), F32),
                 pltpu.VMEM((FSWEEPS, rb, blk, blk), F32),

time: 147 us -> 141 us (0.959)
  the two profiles are of different devices: /device:TPU:1 before, /device:TPU:2 now
where the time goes in v4:
time: 141 us
  Pallas kernels  139 us (99%)
    pallas_call x1, Pallas kernels, local(): pl.pallas_call(make_kernel(n_dom, n_tile, rb, kd, blk, vecs, cap), out_sh...  139 us

profile of v4, /device:TPU:2, one launch (start us, length us, event | category | flops | bytes accessed | tf_op | source)
XLA Modules:
  0.0 141.2 jit_solution(9930060800798166101)
XLA Ops:
  0.6 139.2 %shard_map.86 = (f32[3,128,128]{2,1,0:T(8,128)S(1)}, f32[12,32,128]{2,1,0:T(8,128)S(1)}) custom-call(s32[2,12]{1,0:T(2,128)} %bitcast.4, s32[2,12]{1,0:T(2,128)} %bitcast.5, s32[4,4]{1,0:T(4,128)} %bitcast.3, f32[12,32,128]{2,1,0:T(8,128)} %kry_in.1, f32[3,128,128]{2,1,0:T(8,128)} %diag_in.1, f32[3,128,128]{2,1,0:T(8,128)} %inv_in.1, f32[12,2,128,128]{3,2,1,0:T(8,128)} %coup_in.1), custom_call_target="tpu_custom_call" | custom-call | tf_op jit(solution)/shard_map/pallas_call | solution.py:330
  139.9 0.7 copy.11
  140.6 0.7 copy.12
